TPU v7x, 32 devices: a whole 2x2x4 slice. The times are simulated.
32 devices in a mesh: seq: 4 (over z), uly: 4 (over y, x), rep: 2 (over core).
Axes of the slice: x: 2, y: 2, z: 4, core: 2. Of those that a mesh axis runs over, the one named last changes fastest.
Arguments:
- queries: bfloat16 [4096, 2048], P(('rep', 'seq', 'uly')), parts along dimension 0, may hold values from -6 to 6
- keys: bfloat16 [4096, 2048], P(('rep', 'seq', 'uly')), parts along dimension 0, may hold values from -6 to 6
- values: bfloat16 [4096, 2048], P(('rep', 'seq', 'uly')), parts along dimension 0, may hold values from -6 to 6
- past_outputs: bfloat16 [2, 4096, 2048], P(None, ('rep', 'seq', 'uly')), parts along dimension 1, may hold values from -6 to 6
- dwa_slot: int32 [2], replicated, may hold values from 0 to 63
- dwa_table: float32 [2, 64], replicated, may hold values from 0.1 to 0.6
Outputs:
- mixed: bfloat16 [4096, 2048], P(('rep', 'seq', 'uly')), parts along dimension 0
There are 2 independent parts, one for each index of `rep`. A program takes and returns all parts, laid end to end along the dimension named above; an argument that names none is the same for every part. Nothing has to cross between parts.
All inputs are finite; a program needn't handle non-finite values.
Results may differ from a plain program's by a relative error of at most 0.0034.
Values may be sent and summed in bfloat16 or wider, within the bound.
A program may use at most 64 MiB of HBM per device.

v0:
```python
import jax
import jax.numpy as jnp
from jax import lax
from jax.sharding import PartitionSpec as P

HEAD_DIM = 128


def from_behind(block, axis, distance):
    devices = range(lax.axis_size(axis))
    route = [(i - distance, i) for i in devices if i - distance in devices]
    return lax.ppermute(block, axis, route)


def block_update(state, query_heads, key_heads, value_heads, allowed):
    running, total, accumulated = state
    scores = jnp.einsum("qhd,khd->hqk", query_heads, key_heads, preferred_element_type=jnp.float32)
    scores = scores * (1.0 / HEAD_DIM**0.5)
    scores = jnp.where(allowed, scores, -jnp.inf)
    new_max = jnp.maximum(running, jnp.max(scores, axis=2))
    factor = jnp.exp(running - new_max)
    prob = jnp.exp(scores - new_max[:, :, None])
    total = total * factor + jnp.sum(prob, axis=2)
    weights = prob.astype(jnp.bfloat16)
    update = jnp.einsum("hqk,khd->qhd", weights, value_heads, preferred_element_type=jnp.float32)
    accumulated = accumulated * jnp.transpose(factor)[:, :, None] + update
    return (new_max, total, accumulated)


def shards(queries, keys, values, past_outputs, dwa_slot, dwa_table):
    n_uly = lax.axis_size("uly")
    n_seq = lax.axis_size("seq")
    span_size = min(4, n_seq)
    features = queries.shape[1]
    local_heads = features // n_uly // HEAD_DIM
    query_rows, key_rows, value_rows = (
        lax.all_to_all(queries, "uly", split_axis=1, concat_axis=0, tiled=True),
        lax.all_to_all(keys, "uly", split_axis=1, concat_axis=0, tiled=True),
        lax.all_to_all(values, "uly", split_axis=1, concat_axis=0, tiled=True),
    )
    row_count = query_rows.shape[0]
    split_shape = (row_count, local_heads, HEAD_DIM)
    query_heads = query_rows.reshape(split_shape)
    table_index = jnp.arange(dwa_table.shape[1])
    onehot = (dwa_slot[:, None] == table_index[None, :]).astype(jnp.float32)
    coefs = jnp.dot(onehot, jnp.transpose(dwa_table), precision=lax.Precision.HIGHEST)
    layer_in = jnp.zeros(queries.shape, jnp.float32)
    extra = jnp.zeros(queries.shape, jnp.float32)
    for index in range(past_outputs.shape[0]):
        stored = past_outputs[index].astype(jnp.float32)
        layer_in = layer_in + coefs[index, 0] * stored
        extra = extra + coefs[index, 1] * stored
    running = jnp.full((local_heads, row_count), -jnp.inf, jnp.float32)
    total = jnp.zeros((local_heads, row_count), jnp.float32)
    accumulated = jnp.zeros(split_shape, jnp.float32)
    state = (running, total, accumulated)
    causal = (jnp.arange(row_count)[:, None] >= jnp.arange(row_count)[None, :])[None, :, :]
    state = block_update(
        state, query_heads, key_rows.reshape(split_shape), value_rows.reshape(split_shape), causal
    )
    position = lax.axis_index("seq")
    current = (key_rows, value_rows)
    for offset in range(1, span_size):
        current = from_behind((current[0], current[1]), "seq", 1)
        far_keys = current[0].reshape(split_shape)
        far_values = current[1].reshape(split_shape)

        def take_block(carry, far_keys=far_keys, far_values=far_values):
            return block_update(carry, query_heads, far_keys, far_values, True)

        def keep_block(carry):
            return carry

        state = lax.cond(position >= offset, take_block, keep_block, state)
    running, total, accumulated = state
    attended = accumulated / jnp.transpose(total)[:, :, None]
    attended = attended.astype(jnp.bfloat16).reshape(row_count, local_heads * HEAD_DIM)
    returned = lax.all_to_all(attended, "uly", split_axis=0, concat_axis=1, tiled=True)
    hidden = layer_in + returned.astype(jnp.float32)
    return (hidden + extra).astype(jnp.bfloat16)


def solution(mesh):
    return jax.shard_map(
        shards,
        mesh=mesh,
        in_specs=(
            P(("rep", "seq", "uly"), None),
            P(("rep", "seq", "uly"), None),
            P(("rep", "seq", "uly"), None),
            P(None, ("rep", "seq", "uly"), None),
            P(),
            P(),
        ),
        out_specs=P(("rep", "seq", "uly"), None),
        check_vma=False,
    )
```

profile of v0, /device:TPU:24, one launch (start us, length us, event | category | flops | bytes accessed | tf_op | source)
XLA Modules:
  0.0 108.4 jit_solution(13092285454462107051)
XLA Ops:
  0.0 1.9 %copy.128 = bf16[16,4,8,512]{3,2,0,1:T(8,128)(2,1)} copy(bf16[16,4,8,512]{3,2,1,0:T(8,128)(2,1)} %bitcast.102) | data formatting | bytes 1048576 | tf_op jit(solution)/shard_map/all_to_all | solution.py:38
  1.9 3.7 %all-to-all-start.1 = ((bf16[128,4,512]{2,0,1:T(8,128)(2,1)}), bf16[128,4,512]{2,0,1:T(8,128)(2,1)S(1)}, u32[]{:S(2)}, u32[]{:S(2)}) async-start(bf16[128,4,512]{2,0,1:T(8,128)(2,1)} %bitcast.95), calls=%async_computation.1 | async-start | bytes 1048576 | tf_op jit(solution)/shard_map/all_to_all | solution.py:38
  5.7 1.9 %copy.127 = bf16[16,4,8,512]{3,2,0,1:T(8,128)(2,1)} copy(bf16[16,4,8,512]{3,2,1,0:T(8,128)(2,1)} %bitcast.103) | data formatting | bytes 1048576 | tf_op jit(solution)/shard_map/all_to_all | solution.py:39
  7.5 6.1 %all-to-all-done.1 = bf16[128,4,512]{2,0,1:T(8,128)(2,1)S(1)} async-done(((bf16[128,4,512]{2,0,1:T(8,128)(2,1)}), bf16[128,4,512]{2,0,1:T(8,128)(2,1)S(1)}, u32[]{:S(2)}, u32[]{:S(2)}) %all-to-all-start.1) | async-done | bytes 524320 | tf_op jit(solution)/shard_map/all_to_all | solution.py:38
  13.7 3.5 %all-to-all-start.2 = ((bf16[128,4,512]{2,0,1:T(8,128)(2,1)}), bf16[128,4,512]{2,0,1:T(8,128)(2,1)S(1)}, u32[]{:S(2)}, u32[]{:S(2)}) async-start(bf16[128,4,512]{2,0,1:T(8,128)(2,1)} %bitcast.94), calls=%async_computation.2 | async-start | bytes 1048576 | tf_op jit(solution)/shard_map/all_to_all | solution.py:39
  17.2 1.3 %collective-permute-start = (bf16[512,512]{1,0:T(8,128)(2,1)S(1)}, bf16[512,512]{1,0:T(8,128)(2,1)S(1)}, u32[]{:S(2)}, u32[]{:S(2)}) collective-permute-start(bf16[512,512]{1,0:T(8,128)(2,1)S(1)} %bitcast.99), channel_id=1, source_target_pairs={{0,8},{8,16},{16,24},{1,9},{9,17},{17,25},{2,10},{10,18},{18,26},{... | collective-permute-start | bytes 1572872 | tf_op jit(solution)/shard_map/ppermute | solution.py:12
  18.5 5.9 %all-to-all-done.2 = bf16[128,4,512]{2,0,1:T(8,128)(2,1)S(1)} async-done(((bf16[128,4,512]{2,0,1:T(8,128)(2,1)}), bf16[128,4,512]{2,0,1:T(8,128)(2,1)S(1)}, u32[]{:S(2)}, u32[]{:S(2)}) %all-to-all-start.2) | async-done | bytes 524320 | tf_op jit(solution)/shard_map/all_to_all | solution.py:39
  24.3 1.3 %collective-permute-start.1 = (bf16[512,512]{1,0:T(8,128)(2,1)S(1)}, bf16[512,512]{1,0:T(8,128)(2,1)}, u32[]{:S(2)}, u32[]{:S(2)}) collective-permute-start(bf16[512,512]{1,0:T(8,128)(2,1)S(1)} %bitcast.97), channel_id=1, source_target_pairs={{0,8},{8,16},{16,24},{1,9},{9,17},{17,25},{2,10},{10,18},{18,26},{... | collective-permute-start | bytes 1572872 | tf_op jit(solution)/shard_map/ppermute | solution.py:12
  25.6 0.8 copy.129
  26.5 3.5 %all-to-all-start = ((bf16[128,4,512]{2,0,1:T(8,128)(2,1)}), bf16[128,4,512]{2,0,1:T(8,128)(2,1)S(1)}, u32[]{:S(2)}, u32[]{:S(2)}) async-start(bf16[128,4,512]{2,0,1:T(8,128)(2,1)} %bitcast.96), calls=%async_computation | async-start | bytes 1048576 | tf_op jit(solution)/shard_map/all_to_all | solution.py:37
  30.0 0.1 iota_compare_fusion
  30.1 6.4 %all-to-all-done = bf16[128,4,512]{2,0,1:T(8,128)(2,1)S(1)} async-done(((bf16[128,4,512]{2,0,1:T(8,128)(2,1)}), bf16[128,4,512]{2,0,1:T(8,128)(2,1)S(1)}, u32[]{:S(2)}, u32[]{:S(2)}) %all-to-all-start) | async-done | bytes 524320 | tf_op jit(solution)/shard_map/all_to_all | solution.py:37
  36.5 0.1 reshape.84
  36.6 0.1 reshape.85
  36.8 0.0 collective-permute-done
  36.8 0.0 copy-start.4
  36.8 1.3 %collective-permute-start.2 = (bf16[512,512]{1,0:T(8,128)(2,1)S(1)}, bf16[512,512]{1,0:T(8,128)(2,1)}, u32[]{:S(2)}, u32[]{:S(2)}) collective-permute-start(bf16[512,512]{1,0:T(8,128)(2,1)S(1)} %collective-permute-done), channel_id=1, source_target_pairs={{0,8},{8,16},{16,24},{1,9},{9,17},{17,25},{2,10},{10,18},{18,26},{... | collective-permute-start | bytes 1572872 | tf_op jit(solution)/shard_map/ppermute | solution.py:12
  38.1 7.1 %collective-permute-done.1 = bf16[512,512]{1,0:T(8,128)(2,1)} collective-permute-done((bf16[512,512]{1,0:T(8,128)(2,1)S(1)}, bf16[512,512]{1,0:T(8,128)(2,1)}, u32[]{:S(2)}, u32[]{:S(2)}) %collective-permute-start.1) | collective-permute-done | bytes 524320 | tf_op jit(solution)/shard_map/ppermute | solution.py:12
  45.2 1.3 %collective-permute-start.3 = (bf16[512,512]{1,0:T(8,128)(2,1)}, bf16[512,512]{1,0:T(8,128)(2,1)}, u32[]{:S(2)}, u32[]{:S(2)}) collective-permute-start(bf16[512,512]{1,0:T(8,128)(2,1)} %collective-permute-done.1), channel_id=1, source_target_pairs={{0,8},{8,16},{16,24},{1,9},{9,17},{17,25},{2,10},{10,18},{18,26},{... | collective-permute-start | bytes 1572872 | tf_op jit(solution)/shard_map/ppermute | solution.py:12
  46.5 0.9 fusion.58
  47.4 1.9 %copy-done.1 = f32[4,512,512]{1,2,0:T(8,128)} copy-done((f32[4,512,512]{1,2,0:T(8,128)}, f32[4,512,512]{1,2,0:T(8,128)S(1)}, u32[]{:S(2)}) %copy-start.1) | copy-done | bytes 4194328
  49.4 0.9 fusion.60
  50.3 0.0 copy-done.4
  50.3 6.1 %collective-permute-done.2 = bf16[512,512]{1,0:T(8,128)(2,1)} collective-permute-done((bf16[512,512]{1,0:T(8,128)(2,1)S(1)}, bf16[512,512]{1,0:T(8,128)(2,1)}, u32[]{:S(2)}, u32[]{:S(2)}) %collective-permute-start.2) | collective-permute-done | bytes 524320 | tf_op jit(solution)/shard_map/ppermute | solution.py:12
  56.4 1.3 %collective-permute-start.4 = (bf16[512,512]{1,0:T(8,128)(2,1)}, bf16[512,512]{1,0:T(8,128)(2,1)S(1)}, u32[]{:S(2)}, u32[]{:S(2)}) collective-permute-start(bf16[512,512]{1,0:T(8,128)(2,1)} %collective-permute-done.2), channel_id=1, source_target_pairs={{0,8},{8,16},{16,24},{1,9},{9,17},{17,25},{2,10},{10,18},{18,26},{... | collective-permute-start | bytes 1572872 | tf_op jit(solution)/shard_map/ppermute | solution.py:12
  57.7 9.9 %collective-permute-done.3 = bf16[512,512]{1,0:T(8,128)(2,1)} collective-permute-done((bf16[512,512]{1,0:T(8,128)(2,1)}, bf16[512,512]{1,0:T(8,128)(2,1)}, u32[]{:S(2)}, u32[]{:S(2)}) %collective-permute-start.3) | collective-permute-done | bytes 524320 | tf_op jit(solution)/shard_map/ppermute | solution.py:12
  67.7 1.3 %collective-permute-start.5 = (bf16[512,512]{1,0:T(8,128)(2,1)}, bf16[512,512]{1,0:T(8,128)(2,1)}, u32[]{:S(2)}, u32[]{:S(2)}) collective-permute-start(bf16[512,512]{1,0:T(8,128)(2,1)} %collective-permute-done.3), channel_id=1, source_target_pairs={{0,8},{8,16},{16,24},{1,9},{9,17},{17,25},{2,10},{10,18},{18,26},{... | collective-permute-start | bytes 1572872 | tf_op jit(solution)/shard_map/ppermute | solution.py:12
  69.0 0.1 reshape.86
  69.1 3.8 %fusion.70 = f32[512,4,128]{2,0,1:T(8,128)S(1)} fusion(f32[4,512,512]{1,2,0:T(8,128)} %copy-done.1, f32[4,512]{1,0:T(4,128)S(1)} %get-tuple-element.157, pred[512,512]{0,1:T(8,128)(4,1)S(1)} %iota_compare_fusion, bf16[512,4,128]{2,1,0:T(4,128)(2,1)S(1)} %reshape.86, f32[512,4]{0,1:T(4,128)S(1)} %get-tuple-element.151), kind=kOutput, calls=%fused_computation.66 | convolution fusion | flops 272891904 | bytes 6045696 | tf_op jit(solution)/shard_map/hqk,khd->qhd/dot_general | solution.py:25
  72.9 1.2 %reshape.87 = bf16[512,4,128]{2,1,0:T(4,128)(2,1)S(1)} reshape(bf16[512,512]{1,0:T(8,128)(2,1)} %copy-done.4) | data formatting | bytes 1048576 | tf_op jit(solution)/shard_map/reshape | solution.py:65
  74.0 1.2 %reshape.88 = bf16[512,4,128]{2,1,0:T(4,128)(2,1)S(1)} reshape(bf16[512,512]{1,0:T(8,128)(2,1)} %collective-permute-done.1) | data formatting | bytes 1048576 | tf_op jit(solution)/shard_map/reshape | solution.py:66
  75.2 2.9 %conditional.3 = ((f32[4,512]{1,0:T(4,128)S(1)}, f32[4,512]{1,0:T(4,128)S(1)}, f32[512,4,128]{2,0,1:T(8,128)S(1)})) conditional(s32[]{:T(128)} %convert_element_type.49, (f32[4,512]{1,0:T(4,128)S(1)}, f32[4,512]{1,0:T(4,128)S(1)}, f32[512,4,128]{2,0,1:T(8,128)S(1)}) %tuple.25, (bf16[512,4,128]{2,1,0:T(4,128)(2,1)S(1)}, ...), branch_computations={%region_2.3_spmd, %region_3.6_spmd} | conditional | flops 545789952 | bytes 16384032 | solution.py:74
  75.2 0.7 multiply_reduce_fusion
  76.0 0.7 fusion.1
  76.7 1.4 %fusion.9 = f32[512,4,128]{2,0,1:T(8,128)S(1)} fusion(f32[4,512,512]{1,2,0:T(8,128)S(1)} %get-tuple-element.144, f32[4,512]{1,0:T(4,128)S(1)} %get-tuple-element.162, f32[512,4,128]{2,0,1:T(8,128)S(1)} %get-tuple-element.65, bf16[512,4,128]{2,1,0:T(4,128)(2,1)S(1)} %get-tuple-element.124, f32[512,4]{0,1:T(4,128)S(1)} %get-tuple-element.137), kind=kOutput, calls=%fused_computation.8 | convolution fusion | flops 272105472 | bytes 6832128 | tf_op jit(solution)/shard_map/cond/branch_1_fun/hqk,khd->qhd/dot_general | solution.py:25
  78.2 5.0 %conditional.4 = ((f32[4,512]{1,0:T(4,128)S(1)}, f32[4,512]{1,0:T(4,128)S(1)}, f32[512,4,128]{2,0,1:T(8,128)S(1)})) conditional(s32[]{:T(128)} %convert_element_type.48, (f32[4,512]{1,0:T(4,128)S(1)}, f32[4,512]{1,0:T(4,128)S(1)}, f32[512,4,128]{2,0,1:T(8,128)S(1)}) %get-tuple-element.175, (bf16[512,512]{1,0:T(8,128)(2,1)}, ...), branch_computations={%region_6.7_spmd, %region_7.10_spmd} | conditional | flops 545789952 | bytes 16384032 | solution.py:74
  78.2 1.8 %multiply_reduce_fusion.1 = (f32[4,512]{1,0:T(4,128)S(1)}, f32[4,512,512]{1,2,0:T(8,128)S(1)}) fusion(bf16[512,4,128]{2,1,0:T(4,128)(2,1)S(1)} %get-tuple-element.126, bf16[512,512]{1,0:T(8,128)(2,1)} %get-tuple-element.69), kind=kOutput, calls=%fused_computation.18 | convolution fusion | flops 270530560 | bytes 5251072 | tf_op jit(solution)/shard_map/cond/branch_1_fun/qhd,khd->hqk/dot_general | solution.py:17
  80.0 0.7 fusion.19
  80.7 2.4 %fusion.27 = f32[512,4,128]{2,0,1:T(8,128)S(1)} fusion(f32[4,512,512]{1,2,0:T(8,128)S(1)} %get-tuple-element.146, f32[4,512]{1,0:T(4,128)S(1)} %get-tuple-element.168, f32[512,4,128]{2,0,1:T(8,128)S(1)} %get-tuple-element.71, f32[512,4]{0,1:T(4,128)S(1)} %get-tuple-element.139, bf16[512,512]{1,0:T(8,128)(2,1)} %get-tuple-element.72), kind=kOutput, calls=%fused_computation.25 | convolution fusion | flops 272105472 | bytes 6832128 | tf_op jit(solution)/shard_map/cond/branch_1_fun/hqk,khd->qhd/dot_general | solution.py:25
  83.1 0.0 collective-permute-done.4
  83.1 4.8 %collective-permute-done.5 = bf16[512,512]{1,0:T(8,128)(2,1)} collective-permute-done((bf16[512,512]{1,0:T(8,128)(2,1)}, bf16[512,512]{1,0:T(8,128)(2,1)}, u32[]{:S(2)}, u32[]{:S(2)}) %collective-permute-start.5) | collective-permute-done | bytes 524320 | tf_op jit(solution)/shard_map/ppermute | solution.py:12
  87.9 3.9 %conditional.5 = ((f32[4,512]{1,0:T(4,128)S(1)}, f32[512,4,128]{2,0,1:T(8,128)S(1)})) conditional(s32[]{:T(128)} %convert_element_type.47, (f32[4,512]{1,0:T(4,128)S(1)}, f32[512,4,128]{2,0,1:T(8,128)S(1)}) %tuple.28, (bf16[512,512]{1,0:T(8,128)(2,1)S(1)}, bf16[512,4,128]{2,1,0:T(4,128)(2,1)S(1)}, f32[4,512]{1,0:T(4,128)S(1)}, ...), branch_computations={%region_10.11_spmd, %region_11.14_spmd} | conditional | flops 545789952 | bytes 16367640 | solution.py:74
  87.9 0.7 multiply_reduce_fusion.2
  88.7 0.7 fusion.39
  89.4 2.4 %fusion.47 = f32[512,4,128]{2,0,1:T(8,128)S(1)} fusion(f32[4,512,512]{1,2,0:T(8,128)S(1)} %get-tuple-element.148, f32[4,512]{1,0:T(4,128)S(1)} %get-tuple-element.142, f32[512,4,128]{2,0,1:T(8,128)S(1)} %get-tuple-element.77, f32[512,4]{0,1:T(4,128)S(1)} %get-tuple-element.141, bf16[512,512]{1,0:T(8,128)(2,1)} %get-tuple-element.78), kind=kOutput, calls=%fused_computation.44 | convolution fusion | flops 272105472 | bytes 6832128 | tf_op jit(solution)/shard_map/cond/branch_1_fun/hqk,khd->qhd/dot_general | solution.py:25
  91.8 0.0 copy-start.2
  91.9 0.0 copy-start.5
  91.9 0.3 divide_convert_fusion
  92.2 0.4 copy.60
  92.6 1.0 all_to_all.61
  93.6 3.9 %all-to-all-start.3 = ((bf16[4,128,512]{2,1,0:T(8,128)(2,1)}), bf16[4,128,512]{2,1,0:T(8,128)(2,1)S(1)}, u32[]{:S(2)}, u32[]{:S(2)}) async-start(bf16[4,128,512]{2,1,0:T(8,128)(2,1)} %all_to_all.61), calls=%async_computation.3 | async-start | bytes 1048576 | tf_op jit(solution)/shard_map/all_to_all | solution.py:78
  97.5 0.0 copy-done.2
  97.5 0.1 fusion.92
  97.6 0.3 copy.67
  97.9 0.3 copy.68
  98.2 0.0 copy-done
  98.2 0.0 copy-done.5
  98.2 0.2 fusion.86
  98.4 0.7 fusion.93
  99.0 5.0 %all-to-all-done.3 = bf16[4,128,512]{2,1,0:T(8,128)(2,1)S(1)} async-done(((bf16[4,128,512]{2,1,0:T(8,128)(2,1)}), bf16[4,128,512]{2,1,0:T(8,128)(2,1)S(1)}, u32[]{:S(2)}, u32[]{:S(2)}) %all-to-all-start.3) | async-done | bytes 524320 | tf_op jit(solution)/shard_map/all_to_all | solution.py:78
  104.1 0.1 convert_bitcast_fusion
  104.2 0.3 copy.61
  104.5 2.8 %fusion.77 = bf16[128,2048]{0,1:T(8,128)(2,1)S(1)} fusion(bf16[1,128,2048]{1,2,0:T(8,128)(2,1)S(1)} %copy.67, bf16[1,128,2048]{1,2,0:T(8,128)(2,1)S(1)} %copy.68, f32[128,4,512]{0,2,1:T(8,128)S(1)} %copy.61, f32[]{:T(128)} %bitcast.20, f32[]{:T(128)} %bitcast.19, f32[]{:T(128)} %bitcast.7, f32[]{:T(128)} %bitcast.6), kind=kLoop, calls=%fused_computation.75 | loop fusion | flops 2883584 | bytes 2621456 | tf_op jit(solution)/shard_map/convert_element_type | solution.py:80
  107.4 1.0 copy.62
  (13 shorter events, 0.1 us)
Async XLA Ops:
  0.0 98.2 %copy-start = (f32[2,64]{1,0:T(2,128)S(1)}, f32[2,64]{1,0:T(2,128)}, u32[]{:S(2)}) copy-start(f32[2,64]{1,0:T(2,128)} %param.17) | copy-start | bytes 1540
  0.0 25.6 %copy-start.3 = (bf16[128,2048]{1,0:T(8,128)(2,1)S(1)}, bf16[128,2048]{1,0:T(8,128)(2,1)}, u32[]{:S(2)}) copy-start(bf16[128,2048]{1,0:T(8,128)(2,1)} %param.12) | copy-start | bytes 1572868
  1.9 11.7 %all-to-all-start.1 = ((bf16[128,4,512]{2,0,1:T(8,128)(2,1)}), bf16[128,4,512]{2,0,1:T(8,128)(2,1)S(1)}, u32[]{:S(2)}, u32[]{:S(2)}) async-start(bf16[128,4,512]{2,0,1:T(8,128)(2,1)} %bitcast.95), calls=%async_computation.1 | async-start | bytes 1048576 | tf_op jit(solution)/shard_map/all_to_all | solution.py:38
  13.7 10.7 %all-to-all-start.2 = ((bf16[128,4,512]{2,0,1:T(8,128)(2,1)}), bf16[128,4,512]{2,0,1:T(8,128)(2,1)S(1)}, u32[]{:S(2)}, u32[]{:S(2)}) async-start(bf16[128,4,512]{2,0,1:T(8,128)(2,1)} %bitcast.94), calls=%async_computation.2 | async-start | bytes 1048576 | tf_op jit(solution)/shard_map/all_to_all | solution.py:39
  17.2 19.6 %collective-permute-start = (bf16[512,512]{1,0:T(8,128)(2,1)S(1)}, bf16[512,512]{1,0:T(8,128)(2,1)S(1)}, u32[]{:S(2)}, u32[]{:S(2)}) collective-permute-start(bf16[512,512]{1,0:T(8,128)(2,1)S(1)} %bitcast.99), channel_id=1, source_target_pairs={{0,8},{8,16},{16,24},{1,9},{9,17},{17,25},{2,10},{10,18},{18,26},{... | collective-permute-start | bytes 1572872 | tf_op jit(solution)/shard_map/ppermute | solution.py:12
  24.3 20.9 %collective-permute-start.1 = (bf16[512,512]{1,0:T(8,128)(2,1)S(1)}, bf16[512,512]{1,0:T(8,128)(2,1)}, u32[]{:S(2)}, u32[]{:S(2)}) collective-permute-start(bf16[512,512]{1,0:T(8,128)(2,1)S(1)} %bitcast.97), channel_id=1, source_target_pairs={{0,8},{8,16},{16,24},{1,9},{9,17},{17,25},{2,10},{10,18},{18,26},{... | collective-permute-start | bytes 1572872 | tf_op jit(solution)/shard_map/ppermute | solution.py:12
  26.5 10.0 %all-to-all-start = ((bf16[128,4,512]{2,0,1:T(8,128)(2,1)}), bf16[128,4,512]{2,0,1:T(8,128)(2,1)S(1)}, u32[]{:S(2)}, u32[]{:S(2)}) async-start(bf16[128,4,512]{2,0,1:T(8,128)(2,1)} %bitcast.96), calls=%async_computation | async-start | bytes 1048576 | tf_op jit(solution)/shard_map/all_to_all | solution.py:37
  36.8 13.5 %copy-start.4 = (bf16[512,512]{1,0:T(8,128)(2,1)}, bf16[512,512]{1,0:T(8,128)(2,1)S(1)}, u32[]{:S(2)}) copy-start(bf16[512,512]{1,0:T(8,128)(2,1)S(1)} %collective-permute-done) | copy-start | bytes 1572868
  36.8 19.6 %collective-permute-start.2 = (bf16[512,512]{1,0:T(8,128)(2,1)S(1)}, bf16[512,512]{1,0:T(8,128)(2,1)}, u32[]{:S(2)}, u32[]{:S(2)}) collective-permute-start(bf16[512,512]{1,0:T(8,128)(2,1)S(1)} %collective-permute-done), channel_id=1, source_target_pairs={{0,8},{8,16},{16,24},{1,9},{9,17},{17,25},{2,10},{10,18},{18,26},{... | collective-permute-start | bytes 1572872 | tf_op jit(solution)/shard_map/ppermute | solution.py:12
  45.2 22.5 %collective-permute-start.3 = (bf16[512,512]{1,0:T(8,128)(2,1)}, bf16[512,512]{1,0:T(8,128)(2,1)}, u32[]{:S(2)}, u32[]{:S(2)}) collective-permute-start(bf16[512,512]{1,0:T(8,128)(2,1)} %collective-permute-done.1), channel_id=1, source_target_pairs={{0,8},{8,16},{16,24},{1,9},{9,17},{17,25},{2,10},{10,18},{18,26},{... | collective-permute-start | bytes 1572872 | tf_op jit(solution)/shard_map/ppermute | solution.py:12
  47.4 1.9 %copy-start.1 = (f32[4,512,512]{1,2,0:T(8,128)}, f32[4,512,512]{1,2,0:T(8,128)S(1)}, u32[]{:S(2)}) copy-start(f32[4,512,512]{1,2,0:T(8,128)S(1)} %get-tuple-element.158) | copy-start | bytes 12582916
  56.4 26.7 %collective-permute-start.4 = (bf16[512,512]{1,0:T(8,128)(2,1)}, bf16[512,512]{1,0:T(8,128)(2,1)S(1)}, u32[]{:S(2)}, u32[]{:S(2)}) collective-permute-start(bf16[512,512]{1,0:T(8,128)(2,1)} %collective-permute-done.2), channel_id=1, source_target_pairs={{0,8},{8,16},{16,24},{1,9},{9,17},{17,25},{2,10},{10,18},{18,26},{... | collective-permute-start | bytes 1572872 | tf_op jit(solution)/shard_map/ppermute | solution.py:12
  67.7 20.3 %collective-permute-start.5 = (bf16[512,512]{1,0:T(8,128)(2,1)}, bf16[512,512]{1,0:T(8,128)(2,1)}, u32[]{:S(2)}, u32[]{:S(2)}) collective-permute-start(bf16[512,512]{1,0:T(8,128)(2,1)} %collective-permute-done.3), channel_id=1, source_target_pairs={{0,8},{8,16},{16,24},{1,9},{9,17},{17,25},{2,10},{10,18},{18,26},{... | collective-permute-start | bytes 1572872 | tf_op jit(solution)/shard_map/ppermute | solution.py:12
  91.8 5.7 %copy-start.2 = (bf16[2,128,2048]{2,1,0:T(8,128)(2,1)S(1)}, bf16[2,128,2048]{2,1,0:T(8,128)(2,1)}, u32[]{:S(2)}) copy-start(bf16[2,128,2048]{2,1,0:T(8,128)(2,1)} %param.15) | copy-start | bytes 3145732
  91.9 6.3 %copy-start.5 = (s32[2]{0:T(128)S(1)}, s32[2]{0:T(128)}, u32[]{:S(2)}) copy-start(s32[2]{0:T(128)} %param.16) | copy-start | bytes 28
  93.6 10.4 %all-to-all-start.3 = ((bf16[4,128,512]{2,1,0:T(8,128)(2,1)}), bf16[4,128,512]{2,1,0:T(8,128)(2,1)S(1)}, u32[]{:S(2)}, u32[]{:S(2)}) async-start(bf16[4,128,512]{2,1,0:T(8,128)(2,1)} %all_to_all.61), calls=%async_computation.3 | async-start | bytes 1048576 | tf_op jit(solution)/shard_map/all_to_all | solution.py:78
where the time goes:
time: 109 us; the launch traced here: 108 us
  waiting for transfers between devices  51.5 us (47%)
  starting transfers between devices  22.2 us (20%)
  matrix products  14.4 us (13%)
  local copies, waits for them, and re-layouts  13.4 us (12%)
  other arithmetic  6.49 us (6%)
    ppermute x6, waiting for transfers between devices, from_behind(): return lax.ppermute(block, axis, route)  28 us
    dot_general x4, matrix products, block_update(): jnp.einsum('hqk,khd->qhd', weights, value_heads, preferred_element_type=j...  10.1 us
    ppermute x6, starting transfers between devices, from_behind(): return lax.ppermute(block, axis, route)  7.71 us
    all_to_all x1, waiting for transfers between devices, shards(): lax.all_to_all(queries, 'uly', split_axis=1, concat_axis=0, tiled=True)  6.45 us
    all_to_all x1, waiting for transfers between devices, shards(): lax.all_to_all(keys, 'uly', split_axis=1, concat_axis=0, tiled=True)  6.15 us
    all_to_all x1, waiting for transfers between devices, shards(): lax.all_to_all(values, 'uly', split_axis=1, concat_axis=0, tiled=True)  5.88 us
    all_to_all x1, waiting for transfers between devices, shards(): lax.all_to_all(attended, 'uly', split_axis=0, concat_axis=1, tiled=True)  5.04 us
    dot_general x4, matrix products, block_update(): jnp.einsum('qhd,khd->hqk', query_heads, key_heads, preferred_element_type...  4.16 us
  transfers between devices with their start and end apart: 10, of which 8 were waited for; matrix products, arithmetic and copies ran while one was open for 19% of the time, Pallas kernels for 0%

commit v1 on v0

--- a/solution.py
+++ b/solution.py
@@ -34,7 +34,12 @@
     features = queries.shape[1]
     local_heads = features // n_uly // HEAD_DIM
     query_rows, key_rows, value_rows = (
-        lax.all_to_all(queries, "uly", split_axis=1, concat_axis=0, tiled=True),
+        jnp.concatenate(
+            lax.all_to_all(
+                jnp.stack(jnp.split(queries, lax.axis_size("uly"), axis=1)), "uly", 0, 0
+            ),
+            axis=0,
+        ),
         lax.all_to_all(keys, "uly", split_axis=1, concat_axis=0, tiled=True),
         lax.all_to_all(values, "uly", split_axis=1, concat_axis=0, tiled=True),
     )

time: 109 us -> 109 us (level)
  waiting for transfers between devices: 51.5 us -> 49.6 us
  transfers between devices with their start and end apart: 10 -> 10, of which waited for: 8 -> 8; matrix products, arithmetic and copies ran while one was open for 19% -> 21% of each run, Pallas kernels for 0% -> 0%
where the time goes in v1:
time: 109 us; the launch traced here: 108 us
  waiting for transfers between devices  49.6 us (46%)
  starting transfers between devices  22.2 us (20%)
  matrix products  15.4 us (14%)
  local copies, waits for them, and re-layouts  13.4 us (12%)
  other arithmetic  7.4 us (7%)
    ppermute x6, waiting for transfers between devices, from_behind(): return lax.ppermute(block, axis, route)  27 us
    dot_general x4, matrix products, block_update(): jnp.einsum('hqk,khd->qhd', weights, value_heads, preferred_element_type=j...  10.1 us
    ppermute x6, starting transfers between devices, from_behind(): return lax.ppermute(block, axis, route)  7.71 us
    all_to_all x1, waiting for transfers between devices, shards(): lax.all_to_all(keys, 'uly', split_axis=1, concat_axis=0, tiled=True)  6.15 us
    all_to_all x1, waiting for transfers between devices, shards(): lax.all_to_all(values, 'uly', split_axis=1, concat_axis=0, tiled=True)  5.88 us
    all_to_all x1, waiting for transfers between devices, shards(): lax.all_to_all(jnp.stack(jnp.split(queries, lax.axis_size('uly'), axis=1)...  5.53 us
    dot_general x4, matrix products, block_update(): jnp.einsum('qhd,khd->hqk', query_heads, key_heads, preferred_element_type...  5.19 us
    all_to_all x1, waiting for transfers between devices, shards(): lax.all_to_all(attended, 'uly', split_axis=0, concat_axis=1, tiled=True)  5.08 us
  transfers between devices with their start and end apart: 10, of which 8 were waited for; matrix products, arithmetic and copies ran while one was open for 21% of the time, Pallas kernels for 0%

profile of v1, /device:TPU:24, one launch (start us, length us, event | category | flops | bytes accessed | tf_op | source)
XLA Modules:
  0.0 108.4 jit_solution(8069524321338366013)
XLA Ops:
  0.0 0.0 copy-start
  0.0 1.9 %copy.124 = bf16[16,4,8,512]{3,2,0,1:T(8,128)(2,1)} copy(bf16[16,4,8,512]{3,2,1,0:T(8,128)(2,1)} %bitcast.104) | data formatting | bytes 1048576 | tf_op jit(solution)/shard_map/all_to_all | solution.py:43
  1.9 3.7 %all-to-all-start.1 = ((bf16[128,4,512]{2,0,1:T(8,128)(2,1)}), bf16[128,4,512]{2,0,1:T(8,128)(2,1)S(1)}, u32[]{:S(2)}, u32[]{:S(2)}) async-start(bf16[128,4,512]{2,0,1:T(8,128)(2,1)} %bitcast.99), calls=%async_computation.1 | async-start | bytes 1048576 | tf_op jit(solution)/shard_map/all_to_all | solution.py:43
  5.7 1.9 %copy.123 = bf16[16,4,8,512]{3,2,0,1:T(8,128)(2,1)} copy(bf16[16,4,8,512]{3,2,1,0:T(8,128)(2,1)} %bitcast.105) | data formatting | bytes 1048576 | tf_op jit(solution)/shard_map/all_to_all | solution.py:44
  7.5 6.1 %all-to-all-done.1 = bf16[128,4,512]{2,0,1:T(8,128)(2,1)S(1)} async-done(((bf16[128,4,512]{2,0,1:T(8,128)(2,1)}), bf16[128,4,512]{2,0,1:T(8,128)(2,1)S(1)}, u32[]{:S(2)}, u32[]{:S(2)}) %all-to-all-start.1) | async-done | bytes 524320 | tf_op jit(solution)/shard_map/all_to_all | solution.py:43
  13.7 3.5 %all-to-all-start.2 = ((bf16[128,4,512]{2,0,1:T(8,128)(2,1)}), bf16[128,4,512]{2,0,1:T(8,128)(2,1)S(1)}, u32[]{:S(2)}, u32[]{:S(2)}) async-start(bf16[128,4,512]{2,0,1:T(8,128)(2,1)} %bitcast.98), calls=%async_computation.2 | async-start | bytes 1048576 | tf_op jit(solution)/shard_map/all_to_all | solution.py:44
  17.2 1.3 %collective-permute-start = (bf16[512,512]{1,0:T(8,128)(2,1)S(1)}, bf16[512,512]{1,0:T(8,128)(2,1)S(1)}, u32[]{:S(2)}, u32[]{:S(2)}) collective-permute-start(bf16[512,512]{1,0:T(8,128)(2,1)S(1)} %bitcast.102), channel_id=1, source_target_pairs={{0,8},{8,16},{16,24},{1,9},{9,17},{17,25},{2,10},{10,18},{18,26},{... | collective-permute-start | bytes 1572872 | tf_op jit(solution)/shard_map/ppermute | solution.py:12
  18.5 5.9 %all-to-all-done.2 = bf16[128,4,512]{2,0,1:T(8,128)(2,1)S(1)} async-done(((bf16[128,4,512]{2,0,1:T(8,128)(2,1)}), bf16[128,4,512]{2,0,1:T(8,128)(2,1)S(1)}, u32[]{:S(2)}, u32[]{:S(2)}) %all-to-all-start.2) | async-done | bytes 524320 | tf_op jit(solution)/shard_map/all_to_all | solution.py:44
  24.3 1.3 %collective-permute-start.1 = (bf16[512,512]{1,0:T(8,128)(2,1)S(1)}, bf16[512,512]{1,0:T(8,128)(2,1)}, u32[]{:S(2)}, u32[]{:S(2)}) collective-permute-start(bf16[512,512]{1,0:T(8,128)(2,1)S(1)} %bitcast.100), channel_id=1, source_target_pairs={{0,8},{8,16},{16,24},{1,9},{9,17},{17,25},{2,10},{10,18},{18,26},{... | collective-permute-start | bytes 1572872 | tf_op jit(solution)/shard_map/ppermute | solution.py:12
  25.6 0.0 copy-done.3
  25.7 0.9 pad_maximum_fusion
  26.5 3.5 %all-to-all-start = ((bf16[4,128,512]{2,1,0:T(8,128)(2,1)}), bf16[4,128,512]{2,1,0:T(8,128)(2,1)S(1)}, u32[]{:S(2)}, u32[]{:S(2)}) async-start(bf16[4,128,512]{2,1,0:T(8,128)(2,1)} %pad_maximum_fusion), calls=%async_computation | async-start | bytes 1048576 | tf_op jit(solution)/shard_map/all_to_all | solution.py:38
  30.0 0.1 iota_compare_fusion
  30.1 0.9 reshape.77
  31.0 5.5 %all-to-all-done = bf16[4,128,512]{2,1,0:T(8,128)(2,1)S(1)} async-done(((bf16[4,128,512]{2,1,0:T(8,128)(2,1)}), bf16[4,128,512]{2,1,0:T(8,128)(2,1)S(1)}, u32[]{:S(2)}, u32[]{:S(2)}) %all-to-all-start) | async-done | bytes 524320 | tf_op jit(solution)/shard_map/all_to_all | solution.py:38
  36.6 0.1 reshape_reshape.3
  36.7 0.0 collective-permute-done
  36.7 1.3 %collective-permute-start.2 = (bf16[512,512]{1,0:T(8,128)(2,1)S(1)}, bf16[512,512]{1,0:T(8,128)(2,1)}, u32[]{:S(2)}, u32[]{:S(2)}) collective-permute-start(bf16[512,512]{1,0:T(8,128)(2,1)S(1)} %collective-permute-done), channel_id=1, source_target_pairs={{0,8},{8,16},{16,24},{1,9},{9,17},{17,25},{2,10},{10,18},{18,26},{... | collective-permute-start | bytes 1572872 | tf_op jit(solution)/shard_map/ppermute | solution.py:12
  38.0 7.2 %collective-permute-done.1 = bf16[512,512]{1,0:T(8,128)(2,1)} collective-permute-done((bf16[512,512]{1,0:T(8,128)(2,1)S(1)}, bf16[512,512]{1,0:T(8,128)(2,1)}, u32[]{:S(2)}, u32[]{:S(2)}) %collective-permute-start.1) | collective-permute-done | bytes 524320 | tf_op jit(solution)/shard_map/ppermute | solution.py:12
  45.2 1.3 %collective-permute-start.3 = (bf16[512,512]{1,0:T(8,128)(2,1)}, bf16[512,512]{1,0:T(8,128)(2,1)}, u32[]{:S(2)}, u32[]{:S(2)}) collective-permute-start(bf16[512,512]{1,0:T(8,128)(2,1)} %collective-permute-done.1), channel_id=1, source_target_pairs={{0,8},{8,16},{16,24},{1,9},{9,17},{17,25},{2,10},{10,18},{18,26},{... | collective-permute-start | bytes 1572872 | tf_op jit(solution)/shard_map/ppermute | solution.py:12
  46.5 2.0 %fusion.58 = (f32[4,512]{1,0:T(4,128)S(1)}, f32[4,512,512]{1,2,0:T(8,128)S(1)}) fusion(pred[512,512]{0,1:T(8,128)(4,1)S(1)} %iota_compare_fusion, bf16[512,4,128]{2,1,0:T(4,128)(2,1)} %reshape.77, bf16[512,4,128]{2,1,0:T(4,128)(2,1)S(1)} %reshape_reshape.3), kind=kOutput, calls=%fused_computation.57 | convolution fusion | flops 271579136 | bytes 5513216 | tf_op jit(solution)/shard_map/qhd,khd->hqk/dot_general | solution.py:17
  48.5 1.9 %copy-done.1 = f32[4,512,512]{1,2,0:T(8,128)} copy-done((f32[4,512,512]{1,2,0:T(8,128)}, f32[4,512,512]{1,2,0:T(8,128)S(1)}, u32[]{:S(2)}) %copy-start.1) | copy-done | bytes 4194328
  50.4 0.9 fusion.60
  51.3 5.1 %collective-permute-done.2 = bf16[512,512]{1,0:T(8,128)(2,1)} collective-permute-done((bf16[512,512]{1,0:T(8,128)(2,1)S(1)}, bf16[512,512]{1,0:T(8,128)(2,1)}, u32[]{:S(2)}, u32[]{:S(2)}) %collective-permute-start.2) | collective-permute-done | bytes 524320 | tf_op jit(solution)/shard_map/ppermute | solution.py:12
  56.4 1.3 %collective-permute-start.4 = (bf16[512,512]{1,0:T(8,128)(2,1)}, bf16[512,512]{1,0:T(8,128)(2,1)S(1)}, u32[]{:S(2)}, u32[]{:S(2)}) collective-permute-start(bf16[512,512]{1,0:T(8,128)(2,1)} %collective-permute-done.2), channel_id=1, source_target_pairs={{0,8},{8,16},{16,24},{1,9},{9,17},{17,25},{2,10},{10,18},{18,26},{... | collective-permute-start | bytes 1572872 | tf_op jit(solution)/shard_map/ppermute | solution.py:12
  57.7 9.9 %collective-permute-done.3 = bf16[512,512]{1,0:T(8,128)(2,1)} collective-permute-done((bf16[512,512]{1,0:T(8,128)(2,1)}, bf16[512,512]{1,0:T(8,128)(2,1)}, u32[]{:S(2)}, u32[]{:S(2)}) %collective-permute-start.3) | collective-permute-done | bytes 524320 | tf_op jit(solution)/shard_map/ppermute | solution.py:12
  67.7 1.3 %collective-permute-start.5 = (bf16[512,512]{1,0:T(8,128)(2,1)}, bf16[512,512]{1,0:T(8,128)(2,1)}, u32[]{:S(2)}, u32[]{:S(2)}) collective-permute-start(bf16[512,512]{1,0:T(8,128)(2,1)} %collective-permute-done.3), channel_id=1, source_target_pairs={{0,8},{8,16},{16,24},{1,9},{9,17},{17,25},{2,10},{10,18},{18,26},{... | collective-permute-start | bytes 1572872 | tf_op jit(solution)/shard_map/ppermute | solution.py:12
  69.0 0.1 reshape.78
  69.1 3.8 %fusion.70 = f32[512,4,128]{2,0,1:T(8,128)S(1)} fusion(f32[4,512,512]{1,2,0:T(8,128)} %copy-done.1, f32[4,512]{1,0:T(4,128)S(1)} %get-tuple-element.161, pred[512,512]{0,1:T(8,128)(4,1)S(1)} %iota_compare_fusion, bf16[512,4,128]{2,1,0:T(4,128)(2,1)S(1)} %reshape.78, f32[512,4]{0,1:T(4,128)S(1)} %get-tuple-element.155), kind=kOutput, calls=%fused_computation.66 | convolution fusion | flops 272891904 | bytes 6045696 | tf_op jit(solution)/shard_map/hqk,khd->qhd/dot_general | solution.py:25
  72.9 1.2 %reshape.79 = bf16[512,4,128]{2,1,0:T(4,128)(2,1)S(1)} reshape(bf16[512,512]{1,0:T(8,128)(2,1)} %copy-done.4) | data formatting | bytes 1048576 | tf_op jit(solution)/shard_map/reshape | solution.py:70
  74.0 1.2 %reshape.80 = bf16[512,4,128]{2,1,0:T(4,128)(2,1)S(1)} reshape(bf16[512,512]{1,0:T(8,128)(2,1)} %collective-permute-done.1) | data formatting | bytes 1048576 | tf_op jit(solution)/shard_map/reshape | solution.py:71
  75.2 2.9 %conditional.3 = ((f32[4,512]{1,0:T(4,128)S(1)}, f32[4,512]{1,0:T(4,128)S(1)}, f32[512,4,128]{2,0,1:T(8,128)S(1)})) conditional(s32[]{:T(128)} %convert_element_type.49, (f32[4,512]{1,0:T(4,128)S(1)}, f32[4,512]{1,0:T(4,128)S(1)}, f32[512,4,128]{2,0,1:T(8,128)S(1)}) %tuple.25, (bf16[512,4,128]{2,1,0:T(4,128)(2,1)S(1)}, ...), branch_computations={%region_2.3_spmd, %region_3.6_spmd} | conditional | flops 545789952 | bytes 16384032 | solution.py:79
  75.2 0.7 multiply_reduce_fusion
  76.0 0.7 fusion.1
  76.7 1.4 %fusion.9 = f32[512,4,128]{2,0,1:T(8,128)S(1)} fusion(f32[4,512,512]{1,2,0:T(8,128)S(1)} %get-tuple-element.144, f32[4,512]{1,0:T(4,128)S(1)} %get-tuple-element.166, f32[512,4,128]{2,0,1:T(8,128)S(1)} %get-tuple-element.65, bf16[512,4,128]{2,1,0:T(4,128)(2,1)S(1)} %get-tuple-element.124, f32[512,4]{0,1:T(4,128)S(1)} %get-tuple-element.137), kind=kOutput, calls=%fused_computation.8 | convolution fusion | flops 272105472 | bytes 6832128 | tf_op jit(solution)/shard_map/cond/branch_1_fun/hqk,khd->qhd/dot_general | solution.py:25
  78.1 5.0 %conditional.4 = ((f32[4,512]{1,0:T(4,128)S(1)}, f32[4,512]{1,0:T(4,128)S(1)}, f32[512,4,128]{2,0,1:T(8,128)S(1)})) conditional(s32[]{:T(128)} %convert_element_type.48, (f32[4,512]{1,0:T(4,128)S(1)}, f32[4,512]{1,0:T(4,128)S(1)}, f32[512,4,128]{2,0,1:T(8,128)S(1)}) %get-tuple-element.179, (bf16[512,512]{1,0:T(8,128)(2,1)}, ...), branch_computations={%region_6.7_spmd, %region_7.10_spmd} | conditional | flops 545789952 | bytes 16384032 | solution.py:79
  78.2 1.8 %multiply_reduce_fusion.1 = (f32[4,512]{1,0:T(4,128)S(1)}, f32[4,512,512]{1,2,0:T(8,128)S(1)}) fusion(bf16[512,4,128]{2,1,0:T(4,128)(2,1)S(1)} %get-tuple-element.126, bf16[512,512]{1,0:T(8,128)(2,1)} %get-tuple-element.69), kind=kOutput, calls=%fused_computation.18 | convolution fusion | flops 270530560 | bytes 5251072 | tf_op jit(solution)/shard_map/cond/branch_1_fun/qhd,khd->hqk/dot_general | solution.py:17
  80.0 0.7 fusion.19
  80.7 2.4 %fusion.27 = f32[512,4,128]{2,0,1:T(8,128)S(1)} fusion(f32[4,512,512]{1,2,0:T(8,128)S(1)} %get-tuple-element.146, f32[4,512]{1,0:T(4,128)S(1)} %get-tuple-element.172, f32[512,4,128]{2,0,1:T(8,128)S(1)} %get-tuple-element.71, f32[512,4]{0,1:T(4,128)S(1)} %get-tuple-element.139, bf16[512,512]{1,0:T(8,128)(2,1)} %get-tuple-element.72), kind=kOutput, calls=%fused_computation.25 | convolution fusion | flops 272105472 | bytes 6832128 | tf_op jit(solution)/shard_map/cond/branch_1_fun/hqk,khd->qhd/dot_general | solution.py:25
  83.1 0.0 collective-permute-done.4
  83.1 4.8 %collective-permute-done.5 = bf16[512,512]{1,0:T(8,128)(2,1)} collective-permute-done((bf16[512,512]{1,0:T(8,128)(2,1)}, bf16[512,512]{1,0:T(8,128)(2,1)}, u32[]{:S(2)}, u32[]{:S(2)}) %collective-permute-start.5) | collective-permute-done | bytes 524320 | tf_op jit(solution)/shard_map/ppermute | solution.py:12
  87.9 3.9 %conditional.5 = ((f32[4,512]{1,0:T(4,128)S(1)}, f32[512,4,128]{2,0,1:T(8,128)S(1)})) conditional(s32[]{:T(128)} %convert_element_type.47, (f32[4,512]{1,0:T(4,128)S(1)}, f32[512,4,128]{2,0,1:T(8,128)S(1)}) %tuple.28, (bf16[512,512]{1,0:T(8,128)(2,1)S(1)}, bf16[512,4,128]{2,1,0:T(4,128)(2,1)S(1)}, f32[4,512]{1,0:T(4,128)S(1)}, ...), branch_computations={%region_10.11_spmd, %region_11.14_spmd} | conditional | flops 545789952 | bytes 16367640 | solution.py:79
  87.9 0.7 multiply_reduce_fusion.2
  88.7 0.7 fusion.39
  89.4 2.4 %fusion.47 = f32[512,4,128]{2,0,1:T(8,128)S(1)} fusion(f32[4,512,512]{1,2,0:T(8,128)S(1)} %get-tuple-element.148, f32[4,512]{1,0:T(4,128)S(1)} %get-tuple-element.142, f32[512,4,128]{2,0,1:T(8,128)S(1)} %get-tuple-element.77, f32[512,4]{0,1:T(4,128)S(1)} %get-tuple-element.141, bf16[512,512]{1,0:T(8,128)(2,1)} %get-tuple-element.78), kind=kOutput, calls=%fused_computation.44 | convolution fusion | flops 272105472 | bytes 6832128 | tf_op jit(solution)/shard_map/cond/branch_1_fun/hqk,khd->qhd/dot_general | solution.py:25
  91.8 0.0 copy-start.2
  91.9 0.0 copy-start.5
  91.9 0.3 divide_convert_fusion
  92.2 0.4 copy.58
  92.6 1.0 all_to_all.50
  93.6 3.9 %all-to-all-start.3 = ((bf16[4,128,512]{2,1,0:T(8,128)(2,1)}), bf16[4,128,512]{2,1,0:T(8,128)(2,1)S(1)}, u32[]{:S(2)}, u32[]{:S(2)}) async-start(bf16[4,128,512]{2,1,0:T(8,128)(2,1)} %all_to_all.50), calls=%async_computation.3 | async-start | bytes 1048576 | tf_op jit(solution)/shard_map/all_to_all | solution.py:83
  97.5 0.0 copy-done.2
  97.5 0.1 fusion.92
  97.6 0.3 copy.65
  97.9 0.3 copy.66
  98.2 0.0 copy-done
  98.2 0.0 copy-done.5
  98.2 0.2 fusion.86
  98.4 0.6 fusion.93
  99.0 5.1 %all-to-all-done.3 = bf16[4,128,512]{2,1,0:T(8,128)(2,1)S(1)} async-done(((bf16[4,128,512]{2,1,0:T(8,128)(2,1)}), bf16[4,128,512]{2,1,0:T(8,128)(2,1)S(1)}, u32[]{:S(2)}, u32[]{:S(2)}) %all-to-all-start.3) | async-done | bytes 524320 | tf_op jit(solution)/shard_map/all_to_all | solution.py:83
  104.1 0.1 convert_bitcast_fusion
  104.2 0.3 copy.59
  104.5 2.9 %fusion.77 = bf16[128,2048]{0,1:T(8,128)(2,1)S(1)} fusion(bf16[1,128,2048]{1,2,0:T(8,128)(2,1)S(1)} %copy.65, bf16[1,128,2048]{1,2,0:T(8,128)(2,1)S(1)} %copy.66, f32[128,4,512]{0,2,1:T(8,128)S(1)} %copy.59, f32[]{:T(128)} %bitcast.23, f32[]{:T(128)} %bitcast.22, f32[]{:T(128)} %bitcast.7, f32[]{:T(128)} %bitcast.6), kind=kLoop, calls=%fused_computation.75 | loop fusion | flops 2883584 | bytes 2621456 | tf_op jit(solution)/shard_map/convert_element_type | solution.py:85
  107.4 1.0 copy.60
  (14 shorter events, 0.2 us)
Async XLA Ops:
  0.0 98.2 %copy-start = (f32[2,64]{1,0:T(2,128)S(1)}, f32[2,64]{1,0:T(2,128)}, u32[]{:S(2)}) copy-start(f32[2,64]{1,0:T(2,128)} %param.17) | copy-start | bytes 1540
  0.0 25.6 %copy-start.3 = (bf16[128,2048]{1,0:T(8,128)(2,1)S(1)}, bf16[128,2048]{1,0:T(8,128)(2,1)}, u32[]{:S(2)}) copy-start(bf16[128,2048]{1,0:T(8,128)(2,1)} %param.12) | copy-start | bytes 1572868
  1.9 11.7 %all-to-all-start.1 = ((bf16[128,4,512]{2,0,1:T(8,128)(2,1)}), bf16[128,4,512]{2,0,1:T(8,128)(2,1)S(1)}, u32[]{:S(2)}, u32[]{:S(2)}) async-start(bf16[128,4,512]{2,0,1:T(8,128)(2,1)} %bitcast.99), calls=%async_computation.1 | async-start | bytes 1048576 | tf_op jit(solution)/shard_map/all_to_all | solution.py:43
  13.7 10.7 %all-to-all-start.2 = ((bf16[128,4,512]{2,0,1:T(8,128)(2,1)}), bf16[128,4,512]{2,0,1:T(8,128)(2,1)S(1)}, u32[]{:S(2)}, u32[]{:S(2)}) async-start(bf16[128,4,512]{2,0,1:T(8,128)(2,1)} %bitcast.98), calls=%async_computation.2 | async-start | bytes 1048576 | tf_op jit(solution)/shard_map/all_to_all | solution.py:44
  17.2 19.5 %collective-permute-start = (bf16[512,512]{1,0:T(8,128)(2,1)S(1)}, bf16[512,512]{1,0:T(8,128)(2,1)S(1)}, u32[]{:S(2)}, u32[]{:S(2)}) collective-permute-start(bf16[512,512]{1,0:T(8,128)(2,1)S(1)} %bitcast.102), channel_id=1, source_target_pairs={{0,8},{8,16},{16,24},{1,9},{9,17},{17,25},{2,10},{10,18},{18,26},{... | collective-permute-start | bytes 1572872 | tf_op jit(solution)/shard_map/ppermute | solution.py:12
  24.3 20.9 %collective-permute-start.1 = (bf16[512,512]{1,0:T(8,128)(2,1)S(1)}, bf16[512,512]{1,0:T(8,128)(2,1)}, u32[]{:S(2)}, u32[]{:S(2)}) collective-permute-start(bf16[512,512]{1,0:T(8,128)(2,1)S(1)} %bitcast.100), channel_id=1, source_target_pairs={{0,8},{8,16},{16,24},{1,9},{9,17},{17,25},{2,10},{10,18},{18,26},{... | collective-permute-start | bytes 1572872 | tf_op jit(solution)/shard_map/ppermute | solution.py:12
  26.5 10.0 %all-to-all-start = ((bf16[4,128,512]{2,1,0:T(8,128)(2,1)}), bf16[4,128,512]{2,1,0:T(8,128)(2,1)S(1)}, u32[]{:S(2)}, u32[]{:S(2)}) async-start(bf16[4,128,512]{2,1,0:T(8,128)(2,1)} %pad_maximum_fusion), calls=%async_computation | async-start | bytes 1048576 | tf_op jit(solution)/shard_map/all_to_all | solution.py:38
  36.7 14.6 %copy-start.4 = (bf16[512,512]{1,0:T(8,128)(2,1)}, bf16[512,512]{1,0:T(8,128)(2,1)S(1)}, u32[]{:S(2)}) copy-start(bf16[512,512]{1,0:T(8,128)(2,1)S(1)} %collective-permute-done) | copy-start | bytes 1572868
  36.7 19.7 %collective-permute-start.2 = (bf16[512,512]{1,0:T(8,128)(2,1)S(1)}, bf16[512,512]{1,0:T(8,128)(2,1)}, u32[]{:S(2)}, u32[]{:S(2)}) collective-permute-start(bf16[512,512]{1,0:T(8,128)(2,1)S(1)} %collective-permute-done), channel_id=1, source_target_pairs={{0,8},{8,16},{16,24},{1,9},{9,17},{17,25},{2,10},{10,18},{18,26},{... | collective-permute-start | bytes 1572872 | tf_op jit(solution)/shard_map/ppermute | solution.py:12
  45.2 22.5 %collective-permute-start.3 = (bf16[512,512]{1,0:T(8,128)(2,1)}, bf16[512,512]{1,0:T(8,128)(2,1)}, u32[]{:S(2)}, u32[]{:S(2)}) collective-permute-start(bf16[512,512]{1,0:T(8,128)(2,1)} %collective-permute-done.1), channel_id=1, source_target_pairs={{0,8},{8,16},{16,24},{1,9},{9,17},{17,25},{2,10},{10,18},{18,26},{... | collective-permute-start | bytes 1572872 | tf_op jit(solution)/shard_map/ppermute | solution.py:12
  48.5 2.0 %copy-start.1 = (f32[4,512,512]{1,2,0:T(8,128)}, f32[4,512,512]{1,2,0:T(8,128)S(1)}, u32[]{:S(2)}) copy-start(f32[4,512,512]{1,2,0:T(8,128)S(1)} %get-tuple-element.162) | copy-start | bytes 12582916
  56.4 26.7 %collective-permute-start.4 = (bf16[512,512]{1,0:T(8,128)(2,1)}, bf16[512,512]{1,0:T(8,128)(2,1)S(1)}, u32[]{:S(2)}, u32[]{:S(2)}) collective-permute-start(bf16[512,512]{1,0:T(8,128)(2,1)} %collective-permute-done.2), channel_id=1, source_target_pairs={{0,8},{8,16},{16,24},{1,9},{9,17},{17,25},{2,10},{10,18},{18,26},{... | collective-permute-start | bytes 1572872 | tf_op jit(solution)/shard_map/ppermute | solution.py:12
  67.7 20.3 %collective-permute-start.5 = (bf16[512,512]{1,0:T(8,128)(2,1)}, bf16[512,512]{1,0:T(8,128)(2,1)}, u32[]{:S(2)}, u32[]{:S(2)}) collective-permute-start(bf16[512,512]{1,0:T(8,128)(2,1)} %collective-permute-done.3), channel_id=1, source_target_pairs={{0,8},{8,16},{16,24},{1,9},{9,17},{17,25},{2,10},{10,18},{18,26},{... | collective-permute-start | bytes 1572872 | tf_op jit(solution)/shard_map/ppermute | solution.py:12
  91.8 5.7 %copy-start.2 = (bf16[2,128,2048]{2,1,0:T(8,128)(2,1)S(1)}, bf16[2,128,2048]{2,1,0:T(8,128)(2,1)}, u32[]{:S(2)}) copy-start(bf16[2,128,2048]{2,1,0:T(8,128)(2,1)} %param.15) | copy-start | bytes 3145732
  91.9 6.3 %copy-start.5 = (s32[2]{0:T(128)S(1)}, s32[2]{0:T(128)}, u32[]{:S(2)}) copy-start(s32[2]{0:T(128)} %param.16) | copy-start | bytes 28
  93.6 10.4 %all-to-all-start.3 = ((bf16[4,128,512]{2,1,0:T(8,128)(2,1)}), bf16[4,128,512]{2,1,0:T(8,128)(2,1)S(1)}, u32[]{:S(2)}, u32[]{:S(2)}) async-start(bf16[4,128,512]{2,1,0:T(8,128)(2,1)} %all_to_all.50), calls=%async_computation.3 | async-start | bytes 1048576 | tf_op jit(solution)/shard_map/all_to_all | solution.py:83
